TPU v7x, 32 devices: a whole 2x2x4 slice. The times are simulated.
32 devices in a mesh: image: 4 (over y, x), band: 2 (over core), ga: 4 (over z).
Axes of the slice: x: 2, y: 2, z: 4, core: 2. Of those that a mesh axis runs over, the one named last changes fastest.
Arguments:
- wave_coeffs: bfloat16 [4, 64, 2, 262144], P('image', 'band', None, 'ga'), may hold values from -6 to 6
- occupation: float32 [4, 64], P('image', 'band'), may hold values from 0.003125 to 0.0625
- form_factor: float32 [4, 8, 262144], P(None, None, 'ga'), may hold values from -0.005859375 to 0.005859375
- g_vectors: float32 [3, 262144], P(None, 'ga'), may hold values from -2 to 2
- species: int32 [64], replicated, may hold values from 0 to 3
- proj_count: int32 [4], replicated, may hold values from 1 to 8, as said below
- coupling: float32 [4, 8], replicated, may hold values from 0.5 to 2.5
- positions: float32 [4, 3, 64], P('image'), may hold values from -5.4 to 29.4, as said below
- energy_rest: float32 [4], P('image'), may hold values from -8 to 8
- force_rest: float32 [4, 3, 64], P('image'), may hold values from -6 to 6
- end_positions: float32 [2, 3, 64], replicated, may hold values from -5.4 to 29.4, as said below
- end_energy: float32 [2], replicated, may hold values from -8 to 8
- climb_index: int32 [1], replicated, may hold values from 0 to 3
- tangent_kind: int32 [4], P('image'), may hold values from 0 to 3
Outputs:
- neb_force: float32 [4, 3, 64], P('image')
- energy: float32 [4], P('image')
Inputs may be any that keep to these rules, and one draw needn't show every extreme that they name: `proj_count`: each species has between 1 and 8 live projector slots, and some species has exactly 8. `positions`: atom coordinates in bohr. `end_positions`: atom coordinates in bohr.
All inputs are finite; a program needn't handle non-finite values.
Results may differ from a plain program's by a relative error of at most 0.0003.
The roundings to bfloat16 on the way count: a program that leaves them out, or rounds other values in their place, can miss the bound.
Values sent between devices are 32-bit elements; how exact they have to be, the bound alone decides.
A program may use at most 128 MiB of HBM per device.

v0:
```python
import math

import jax
import jax.numpy as jnp
from jax import lax
from jax.experimental import pallas as pl
from jax.experimental.pallas import tpu as pltpu
from jax.sharding import PartitionSpec as P

ATOMS = 64
PMAX = 8
SPECIES = 4


spring_constant = 5.0


def passed_along(array, axis, by):
    length = lax.axis_size(axis)
    pairs = [(i, i + by) for i in range(length) if 0 <= i + by < length]
    return lax.ppermute(array, axis, pairs)


def atom_tables(species, proj_count, coupling):
    is_species = (species[:, None] == jnp.arange(SPECIES)[None, :]).astype(jnp.float32)
    is_live = (jnp.arange(PMAX)[None, :] < proj_count[:, None]).astype(jnp.float32)
    species_mask = is_species[:, :, None] * is_live[None, :, :]
    strength = jnp.sum(species_mask * coupling[None, :, :], axis=1)
    return (species_mask, strength)


SIN_HALF = (0.7071067780965931, -0.02946276693049568, 0.00036827213876565137, -2.1885830267998076e-06, 7.194201360627222e-09)
COS_HALF = (-1.4142134949348355, 0.17677635430234293, -0.003682571658574129, 3.061195661905538e-05, -1.2786908538293617e-07)
TURN_HIGH = 6.28125
TURN_LOW = 0.001935307179586232
ROUNDER = 12582912.0
SUB = 1024
BLOCK = 8192
GROUP = 8


def horner(coefs, z):
    total = coefs[-1] * z + coefs[-2]
    for coef in coefs[-3::-1]:
        total = total * z + coef
    return total


def cos_and_minus_sin(phases):
    turns = (phases * 0.15915494309189535 + ROUNDER) - ROUNDER
    r = (phases - turns * TURN_HIGH) - turns * TURN_LOW
    z = r * r
    half_sin = r * horner(SIN_HALF, z)
    return (1.0 - half_sin * half_sin, half_sin * horner(COS_HALF, z))


def sums_kernel(spec_ref, w_ref, ff_ref, g_ref, pos_ref, live_ref, out_ref,
                acc, rad, stk, prj, trig):
    step = pl.program_id(0)
    rows = w_ref.shape[0]
    bands = rows // 2
    block = w_ref.shape[1]
    sub = stk.shape[1]
    groups = prj.shape[0]
    half = GROUP * PMAX

    @pl.when(step == 0)
    def _():
        acc[...] = jnp.zeros_like(acc)

    def wide(x):
        return jnp.concatenate([x] * (sub // 128), axis=1)

    def body(t, carry):
        lanes = pl.ds(pl.multiple_of(t * sub, sub), sub)
        for s in range(SPECIES):
            rad[s] = ff_ref[s, :, lanes] * wide(live_ref[s])
        w = w_ref[:, lanes]
        stk[0:rows, :] = w
        for c in range(3):
            stk[(c + 1) * rows : (c + 2) * rows, :] = (
                g_ref[c : c + 1, lanes] * w.astype(jnp.float32)
            ).astype(jnp.bfloat16)

        def multiply(j):
            acc[j] += lax.dot_general(
                prj[j], stk[...], (((1,), (1,)), ((), ())), preferred_element_type=jnp.float32
            )

        for j in range(groups):
            mine = slice(j * GROUP, (j + 1) * GROUP)
            phases = wide(pos_ref[0, mine, :]) * g_ref[0:1, lanes]
            phases = phases + wide(pos_ref[1, mine, :]) * g_ref[1:2, lanes]
            phases = phases + wide(pos_ref[2, mine, :]) * g_ref[2:3, lanes]
            cosine, minus_sine = cos_and_minus_sin(phases)
            trig[j, 0] = cosine
            trig[j, 1] = minus_sine
            for i in range(0, GROUP, 2):
                first = rad[spec_ref[j * GROUP + i]]
                second = rad[spec_ref[j * GROUP + i + 1]]
                for part in range(2):
                    pair = jnp.concatenate(
                        [first * trig[j, part, i : i + 1, :],
                         second * trig[j, part, i + 1 : i + 2, :]], axis=0)
                    at = part * half + i * PMAX
                    prj[j, at : at + 2 * PMAX, :] = pair.astype(jnp.bfloat16)
            if j > 0:
                multiply(j - 1)
        multiply(groups - 1)
        return carry

    lax.fori_loop(0, block // sub, body, 0)

    @pl.when(step == pl.num_programs(0) - 1)
    def _():
        for j in range(groups):
            real = acc[j, :half, :]
            imag = acc[j, half:, :]
            here = slice(j * half, (j + 1) * half)
            out_ref[here, 0:bands] = 2.0 * (real[:, :bands] + imag[:, bands:rows])
            for c in range(1, 4):
                out_ref[here, c * bands : (c + 1) * bands] = 2.0 * (
                    imag[:, c * rows : c * rows + bands]
                    - real[:, c * rows + bands : (c + 1) * rows]
                )


def projector_sums(waves, form_factor, g_vectors, species, proj_count, atom_pos):
    bands, _, length = waves.shape
    atoms = species.shape[0]
    w = jnp.swapaxes(waves, 0, 1).reshape(2 * bands, length)
    block = math.gcd(length, BLOCK)
    sub = math.gcd(block, SUB)
    groups = atoms // GROUP
    live = (jnp.arange(PMAX)[None, :] < proj_count[:, None]).astype(jnp.float32)
    live = jnp.broadcast_to(live[:, :, None], (SPECIES, PMAX, 128))
    pos = jnp.broadcast_to(atom_pos[:, :, None], (3, atoms, 128))
    grid_spec = pltpu.PrefetchScalarGridSpec(
        num_scalar_prefetch=1,
        grid=(length // block,),
        in_specs=[
            pl.BlockSpec((2 * bands, block), lambda i, sp: (0, i)),
            pl.BlockSpec((SPECIES, PMAX, block), lambda i, sp: (0, 0, i)),
            pl.BlockSpec((3, block), lambda i, sp: (0, i)),
            pl.BlockSpec((3, atoms, 128), lambda i, sp: (0, 0, 0)),
            pl.BlockSpec((SPECIES, PMAX, 128), lambda i, sp: (0, 0, 0)),
        ],
        out_specs=pl.BlockSpec((atoms * PMAX, 4 * bands), lambda i, sp: (0, 0)),
        scratch_shapes=[
            pltpu.VMEM((groups, 2 * GROUP * PMAX, 8 * bands), jnp.float32),
            pltpu.VMEM((SPECIES, PMAX, sub), jnp.float32),
            pltpu.VMEM((8 * bands, sub), jnp.bfloat16),
            pltpu.VMEM((groups, 2 * GROUP * PMAX, sub), jnp.bfloat16),
            pltpu.VMEM((groups, 2, GROUP, sub), jnp.float32),
        ],
    )
    return pl.pallas_call(
        sums_kernel,
        grid_spec=grid_spec,
        out_shape=jax.ShapeDtypeStruct((atoms * PMAX, 4 * bands), jnp.float32),
        compiler_params=pltpu.CompilerParams(vmem_limit_bytes=48 * 1024 * 1024),
    )(species, w, form_factor, g_vectors, pos, live)


def nonlocal_terms(proj_sums, occupied, strength):
    band_count = occupied.shape[0]
    atom_count = strength.shape[0]
    intersect = proj_sums[:, :band_count]
    weighted = intersect * occupied[None, :]
    energy_part = jnp.sum(strength.reshape(-1) * jnp.sum(weighted * intersect, axis=1))
    forces = []
    for axis_num in range(3):
        slope = proj_sums[:, (axis_num + 1) * band_count : (axis_num + 2) * band_count]
        per_row = jnp.sum(weighted * slope, axis=1).reshape(atom_count, PMAX)
        forces.append(-2.0 * jnp.sum(strength * per_row, axis=1))
    return (energy_part, jnp.stack(forces, axis=0))


def neb_project(
    force, here, prev_pos, next_pos, energy, prev_energy, next_energy, tangent_kind, is_climb
):
    to_next = next_pos - here
    from_prev = here - prev_pos
    rise_next = jnp.abs(next_energy - energy)
    rise_prev = jnp.abs(prev_energy - energy)
    larger = jnp.maximum(rise_next, rise_prev)
    smaller = jnp.minimum(rise_next, rise_prev)
    rising = next_energy > prev_energy
    weight_next = 1.0 + jnp.where(rising, larger, smaller)
    weight_prev = 1.0 + jnp.where(rising, smaller, larger)
    stiff_next = spring_constant * (1.0 + jax.nn.sigmoid(0.5 * (next_energy + energy)))
    stiff_prev = spring_constant * (1.0 + jax.nn.sigmoid(0.5 * (prev_energy + energy)))
    length_next = jnp.sqrt(jnp.sum(to_next * to_next, axis=(1, 2)) + 1.0)
    length_prev = jnp.sqrt(jnp.sum(from_prev * from_prev, axis=(1, 2)) + 1.0)
    upwind = weight_next[:, None, None] * to_next + weight_prev[:, None, None] * from_prev
    forward = to_next / length_next[:, None, None]
    backward = from_prev / length_prev[:, None, None]
    kind = tangent_kind[:, None, None]
    tangent = jnp.where(
        kind == 0,
        upwind,
        jnp.where(kind == 1, forward + backward, jnp.where(kind == 2, forward, backward)),
    )
    unit_tangent = tangent / jnp.sqrt(jnp.sum(tangent * tangent, axis=(1, 2)) + 1.0)[:, None, None]
    along = jnp.sum(force * unit_tangent, axis=(1, 2))[:, None, None]
    climbing = force - 2.0 * along * unit_tangent
    regular = (
        force
        - along * unit_tangent
        + (stiff_next * length_next - stiff_prev * length_prev)[:, None, None] * unit_tangent
    )
    return jnp.where(is_climb[:, None, None], climbing, regular)


def per_device(
    wave_coeffs,
    occupation,
    form_factor,
    g_vectors,
    species,
    proj_count,
    coupling,
    positions,
    energy_rest,
    force_rest,
    end_positions,
    end_energy,
    climb_index,
    tangent_kind,
):
    species_mask, strength = atom_tables(species, proj_count, coupling)
    occupied = occupation[0]
    local_atoms = ATOMS // lax.axis_size("ga")
    sums = projector_sums(
        wave_coeffs[0], form_factor, g_vectors, species, proj_count, positions[0]
    )
    proj_sums = lax.psum_scatter(sums, "ga", scatter_dimension=0, tiled=True)
    first_local = lax.axis_index("ga") * local_atoms
    strength_part = lax.dynamic_slice_in_dim(strength, first_local, local_atoms, 0)
    energy_part, force_part = nonlocal_terms(proj_sums, occupied, strength_part)
    force_full = lax.dynamic_update_slice_in_dim(
        jnp.zeros((3, ATOMS), jnp.float32), force_part, first_local, 1
    )
    force_nl, energy_nl = lax.psum((force_full, energy_part), ("band", "ga"))
    energy = energy_rest + energy_nl
    force = force_rest + force_nl[None, :, :]
    image_index = lax.axis_index("image")
    image_count = lax.axis_size("image")
    prev_pos, prev_energy = passed_along((positions, energy), "image", 1)
    next_pos, next_energy = passed_along((positions, energy), "image", -1)
    at_start = image_index == 0
    at_end = image_index == image_count - 1
    prev_pos = jnp.where(at_start, end_positions[:1], prev_pos)
    prev_energy = jnp.where(at_start, end_energy[:1], prev_energy)
    next_pos = jnp.where(at_end, end_positions[1:], next_pos)
    next_energy = jnp.where(at_end, end_energy[1:], next_energy)
    is_climb = climb_index == image_index
    neb_force = neb_project(
        force,
        positions,
        prev_pos,
        next_pos,
        energy,
        prev_energy,
        next_energy,
        tangent_kind,
        is_climb,
    )
    return (neb_force, energy)


def solution(mesh):
    in_specs = (
        P("image", "band", None, "ga"),
        P("image", "band"),
        P(None, None, "ga"),
        P(None, "ga"),
        P(),
        P(),
        P(),
        P("image", None, None),
        P("image"),
        P("image", None, None),
        P(),
        P(),
        P(),
        P("image"),
    )
    out_specs = (P("image", None, None), P("image"))
    return jax.shard_map(
        per_device, mesh=mesh, in_specs=in_specs, out_specs=out_specs, check_vma=False
    )
```

profile of v0, /device:TPU:0, one launch (start us, length us, event | category | flops | bytes accessed | tf_op | source)
XLA Modules:
  0.0 185.0 jit_solution(859380208025803431)
XLA Ops:
  7.2 1.3 collective-permute-start.2
  8.5 5.5 %collective-permute-start.3 = (f32[1,3,64]{2,0,1:T(1,128)}, f32[1,3,64]{2,0,1:T(1,128)S(1)}, u32[]{:S(2)}, u32[]{:S(2)}) collective-permute-start(f32[1,3,64]{2,0,1:T(1,128)} %param.21), channel_id=1, source_target_pairs={{0,8},{8,16},{16,24},{1,9},{9,17},{17,25},{2,10},{10,18},{18,26},{... | collective-permute-start | bytes 2312 | tf_op jit(solution)/shard_map/ppermute | solution.py:21
  14.0 0.7 copy.28
  14.7 0.7 fusion.5
  15.4 11.3 %copy.20 = bf16[2,32,65536]{2,1,0:T(8,128)(2,1)} copy(bf16[2,32,65536]{2,0,1:T(2,128)(2,1)} %bitcast.30) | data formatting | bytes 16777216 | tf_op jit(solution)/shard_map/transpose | solution.py:131
  26.8 0.1 broadcast_in_dim.72.pos_ref
  27.0 94.8 %shard_map.149 = f32[512,128]{1,0:T(8,128)} custom-call(s32[64]{0:T(128)S(1)} %copy-done.1, bf16[64,65536]{1,0:T(8,128)(2,1)} %bitcast.29, f32[4,8,65536]{2,1,0:T(8,128)} %ff_ref.1, f32[3,65536]{1,0:T(4,128)S(1)} %copy-done, f32[3,64,128]{2,1,0:T(8,128)S(1)} %broadcast_in_dim.72.pos_ref, f32[4,8,128]{2,1,0:T(8,128)S(1)} %broadcast_in_dim.73.live_ref), custom_call_target="tpu_custom_call" | custom-call | tf_op jit(solution)/shard_map/pallas_call | solution.py:157
  122.5 0.6 fusion.10
  124.6 0.6 multiply_reduce_fusion.8
  126.6 17.2 %reduce-scatter.2.cloned.1.call-done = f32[128,128]{1,0:T(8,128)} async-done(((f32[512,128]{1,0:T(8,128)}), f32[128,128]{1,0:T(8,128)}) %reduce-scatter.2.cloned.1.call-update) | async-done | bytes 65552 | tf_op jit(solution)/shard_map/reduce_scatter | solution.py:237
  143.7 1.2 fusion
  144.9 0.1 reshape.172
  145.2 0.1 copy.22
  145.3 0.1 copy.23
  145.5 0.1 copy.25
  145.6 0.7 multiply_reduce_fusion.4
  146.3 0.2 dynamic_update_slice.4
  146.5 14.3 %all-reduce = (f32[1]{0:T(128)}, f32[1,3,64]{2,0,1:T(1,128)S(1)}) all-reduce(f32[1]{0:T(128)} %bitcast.12, f32[1,3,64]{2,0,1:T(1,128)S(1)} %dynamic_update_slice.4), channel_id=1, replica_groups=mesh['image'=4,'band'=2,'ga'=4] {'band','ga'}, use_global_device_ids=true, to_apply=%region_11.0 | all-reduce | flops 193 | bytes 1544 | tf_op jit(solution)/shard_map/psum | solution.py:244
  161.5 4.6 %collective-permute-start.1 = (f32[1]{0:T(128)}, f32[1]{0:T(128)}, u32[]{:S(2)}, u32[]{:S(2)}) collective-permute-start(f32[1]{0:T(128)} %add.67), channel_id=1, source_target_pairs={{0,8},{8,16},{16,24},{1,9},{9,17},{17,25},{2,10},{10,18},{18,26},{... | collective-permute-start | bytes 20 | tf_op jit(solution)/shard_map/ppermute | solution.py:21
  166.1 1.3 collective-permute-start
  168.6 2.9 %collective-permute-done = f32[1]{0:T(128)} collective-permute-done((f32[1]{0:T(128)}, f32[1]{0:T(128)}, u32[]{:S(2)}, u32[]{:S(2)}) %collective-permute-start) | collective-permute-done | bytes 36 | tf_op jit(solution)/shard_map/ppermute | solution.py:21
  173.0 0.6 multiply_reduce_fusion.6
  174.4 0.7 multiply_reduce_fusion.5
  175.8 1.3 broadcast_select_fusion.5
  (33 shorter events, 0.6 us)
Async XLA Ops:
  7.2 136.6 %reduce-scatter.2.cloned.1.call-start = ((), (), s32[]{:S(2)}) async-start(), calls=%async_computation.1 | async-start | bytes 327680 | tf_op jit(solution)/shard_map/reduce_scatter | solution.py:237
  7.2 117.3 %collective-permute-start.2 = (f32[1,3,64]{2,0,1:T(1,128)}, f32[1,3,64]{2,0,1:T(1,128)S(1)}, u32[]{:S(2)}, u32[]{:S(2)}) collective-permute-start(f32[1,3,64]{2,0,1:T(1,128)} %param.21), channel_id=1, source_target_pairs={{8,0},{16,8},{24,16},{9,1},{17,9},{25,17},{10,2},{18,10},{26,18},{... | collective-permute-start | bytes 2312 | tf_op jit(solution)/shard_map/ppermute | solution.py:21
  8.5 116.0 %collective-permute-start.3 = (f32[1,3,64]{2,0,1:T(1,128)}, f32[1,3,64]{2,0,1:T(1,128)S(1)}, u32[]{:S(2)}, u32[]{:S(2)}) collective-permute-start(f32[1,3,64]{2,0,1:T(1,128)} %param.21), channel_id=1, source_target_pairs={{0,8},{8,16},{16,24},{1,9},{9,17},{17,25},{2,10},{10,18},{18,26},{... | collective-permute-start | bytes 2312 | tf_op jit(solution)/shard_map/ppermute | solution.py:21
  15.4 11.5 %copy-start = (f32[3,65536]{1,0:T(4,128)S(1)}, f32[3,65536]{1,0:T(4,128)}, u32[]{:S(2)}) copy-start(f32[3,65536]{1,0:T(4,128)} %g_ref.1) | copy-start | bytes 2359300
  15.4 11.5 %copy-start.1 = (s32[64]{0:T(128)S(1)}, s32[64]{0:T(128)}, u32[]{:S(2)}) copy-start(s32[64]{0:T(128)} %spec_ref.1) | copy-start | bytes 772
  26.9 95.6 %copy-start.5 = (f32[2]{0:T(128)S(1)}, f32[2]{0:T(128)}, u32[]{:S(2)}) copy-start(f32[2]{0:T(128)} %param.25) | copy-start | bytes 28
  26.9 96.2 %copy-start.4 = (f32[4,8]{1,0:T(4,128)S(1)}, f32[4,8]{1,0:T(4,128)}, u32[]{:S(2)}) copy-start(f32[4,8]{1,0:T(4,128)} %param.20) | copy-start | bytes 388
  26.9 97.6 %copy-start.2 = (f32[1,3,64]{2,0,1:T(1,128)S(1)}, f32[1,3,64]{2,0,1:T(1,128)}, u32[]{:S(2)}) copy-start(f32[1,3,64]{2,0,1:T(1,128)} %param.21) | copy-start | bytes 2308
  27.0 97.6 %copy-start.3 = (f32[2,3,64]{2,0,1:T(2,128)S(1)}, f32[2,3,64]{2,0,1:T(2,128)}, u32[]{:S(2)}) copy-start(f32[2,3,64]{2,0,1:T(2,128)} %param.24) | copy-start | bytes 4612
  27.0 116.8 %copy-start.7 = (f32[1,32]{1,0:T(1,128)S(1)}, f32[1,32]{1,0:T(1,128)}, u32[]{:S(2)}) copy-start(f32[1,32]{1,0:T(1,128)} %param.15) | copy-start | bytes 388
  27.0 147.4 %copy-start.6 = (f32[1,3,64]{2,0,1:T(1,128)S(1)}, f32[1,3,64]{2,0,1:T(1,128)}, u32[]{:S(2)}) copy-start(f32[1,3,64]{2,0,1:T(1,128)} %param.23) | copy-start | bytes 2308
  161.5 5.9 %collective-permute-start.1 = (f32[1]{0:T(128)}, f32[1]{0:T(128)}, u32[]{:S(2)}, u32[]{:S(2)}) collective-permute-start(f32[1]{0:T(128)} %add.67), channel_id=1, source_target_pairs={{0,8},{8,16},{16,24},{1,9},{9,17},{17,25},{2,10},{10,18},{18,26},{... | collective-permute-start | bytes 20 | tf_op jit(solution)/shard_map/ppermute | solution.py:21
  166.1 5.4 %collective-permute-start = (f32[1]{0:T(128)}, f32[1]{0:T(128)}, u32[]{:S(2)}, u32[]{:S(2)}) collective-permute-start(f32[1]{0:T(128)} %add.67), channel_id=1, source_target_pairs={{8,0},{16,8},{24,16},{9,1},{17,9},{25,17},{10,2},{18,10},{26,18},{... | collective-permute-start | bytes 20 | tf_op jit(solution)/shard_map/ppermute | solution.py:21
Sparse Core Ops, SparseCore 0:
  122.0 21.7 reduce-scatter.1
where the time goes:
time: 185 us
  Pallas kernels  94.8 us (51%)
  between operations  23.4 us (13%)
  waiting for transfers between devices  20.1 us (11%)
  blocking collectives  14.3 us (8%)
  local copies, waits for them, and re-layouts  13.6 us (7%)
  starting transfers between devices  12.8 us (7%)
  other arithmetic  5.94 us (3%)
    pallas_call x1, Pallas kernels, projector_sums(): pl.pallas_call(sums_kernel, grid_spec=grid_spec, out_shape=jax.ShapeDtype...  94.8 us
    reduce_scatter x1, waiting for transfers between devices, per_device(): proj_sums = lax.psum_scatter(sums, 'ga', scatter_dimension=0, tiled=True)  17.2 us
    psum x1, blocking collectives, per_device(): force_nl, energy_nl = lax.psum((force_full, energy_part), ('band', 'ga'))  14.3 us
    ppermute x4, starting transfers between devices, passed_along(): return lax.ppermute(array, axis, pairs)  12.7 us
    transpose x1, local copies, waits for them, and re-layouts, projector_sums(): w = jnp.swapaxes(waves, 0, 1).reshape(2 * bands, length)  11.3 us
  transfers between devices with their start and end apart: 5, of which 2 were waited for; matrix products, arithmetic and copies ran while one was open for 8% of the time, Pallas kernels for 51%

commit v1 on v0

v1 whole, which is shorter than its diff:
```python
import functools

import jax
import jax.numpy as jnp
from jax import lax
from jax.experimental import pallas as pl
from jax.experimental.pallas import tpu as pltpu
from jax.sharding import PartitionSpec as P

SPRING = 5.0
SIN_HALF = (0.7071067780965931, -0.02946276693049568, 0.00036827213876565137, -2.1885830267998076e-06, 7.194201360627222e-09)
COS_HALF = (-1.4142134949348355, 0.17677635430234293, -0.003682571658574129, 3.061195661905538e-05, -1.2786908538293617e-07)
TURN_HIGH = 6.28125
TURN_LOW = 0.001935307179586232
ROUNDER = 12582912.0
LANE = 128
WIDE = 256
CHUNKS = 8
MESH = pl.DeviceIdType.MESH
F32 = jnp.float32
BF16 = jnp.bfloat16


def horner(coefs, z):
    total = coefs[-1] * z + coefs[-2]
    for coef in coefs[-3::-1]:
        total = total * z + coef
    return total


def cos_and_minus_sin(phases):
    turns = (phases * 0.15915494309189535 + ROUNDER) - ROUNDER
    r = (phases - turns * TURN_HIGH) - turns * TURN_LOW
    z = r * r
    half_sin = r * horner(SIN_HALF, z)
    return (1.0 - half_sin * half_sin, half_sin * horner(COS_HALF, z))


def iota(shape, dim):
    return lax.broadcasted_iota(jnp.int32, shape, dim)


def column(row, start, rows):
    n = row.shape[1]
    here = iota((rows, n), 1) == iota((rows, n), 0) + start
    return jnp.sum(jnp.where(here, row, 0.0), axis=1, keepdims=True)


def row_of(col, start):
    rows = col.shape[0]
    here = iota((rows, LANE), 1) == iota((rows, LANE), 0) + start
    return jnp.sum(jnp.where(here, col, 0.0), axis=0, keepdims=True)


def total(x):
    return jnp.sum(jnp.sum(x, axis=1, keepdims=True), axis=0, keepdims=True)


def kernel(
    w_hbm, occ_hbm, ff_hbm, g_hbm, spec_hbm, count_hbm, coup_hbm, pos_hbm, erest_hbm, frest_hbm,
    endp_hbm, ende_hbm, climb_hbm, kind_hbm,
    force_out, energy_out,
    raw_other, raw_own, w_send, w_all, ff, g, pos, coup, occ, erest, frest, endp, ende,
    spec, count, climb, kind,
    pos_wide, live, strength, occ_part, occ_peer, trig_a, trig_b, rad_a, rad_b,
    part, part_peer, z_send, z_recv, msg, msgs,
    small_sem, other_sem, own_sem, ff_sem, g_sem, w_send_sem, w_recv_sem, occ_sem,
    part_sems, z_sems, msg_send_sem, msg_recv_sem,
):
    image, band, ga = (lax.axis_index(a) for a in ("image", "band", "ga"))
    n_image, n_band, n_ga = (lax.axis_size(a) for a in ("image", "band", "ga"))
    group = n_band * n_ga
    side = lax.rem(band, 2)
    peer = band + 1 - 2 * side
    bands = w_hbm.shape[0]
    blocks, tiles = raw_own.shape[0], raw_own.shape[1]
    species, slots = coup.shape
    atoms = pos.shape[2]
    half_len = ff.shape[2]
    n_wide = half_len // WIDE
    step_tiles = tiles // CHUNKS
    owners = part.shape[0]
    own_atoms = atoms // owners
    own_rows = part.shape[1]
    n_groups = atoms // 8

    small = [
        (occ_hbm, occ), (coup_hbm, coup), (pos_hbm, pos), (erest_hbm, erest), (frest_hbm, frest), (endp_hbm, endp),
        (ende_hbm, ende), (spec_hbm, spec), (count_hbm, count), (climb_hbm, climb), (kind_hbm, kind),
    ]
    small = [pltpu.make_async_copy(a, b, small_sem.at[i]) for i, (a, b) in enumerate(small)]

    def wave_copies(raw, which, c, count, sem):
        at = which * tiles + c * count
        return [
            pltpu.make_async_copy(
                w_hbm.at[n, pl.ds(at, count)],
                raw.at[n // 8, pl.ds(c * count, count), pl.ds(2 * (n % 8), 2), :],
                sem,
            )
            for n in range(bands)
        ]

    def start_other(c):
        for copy in wave_copies(raw_other, 1 - side, c, step_tiles, other_sem.at[c]):
            copy.start()

    mine = pl.ds(pl.multiple_of(side * half_len, WIDE), half_len)
    ff_copy = pltpu.make_async_copy(ff_hbm.at[:, :, mine], ff, ff_sem)
    g_copy = pltpu.make_async_copy(g_hbm.at[:, mine], g, g_sem)
    start_other(0)
    for copy in small:
        copy.start()
    start_other(1)

    barrier = pltpu.get_barrier_semaphore()
    for d_image in (0, 1, n_image - 1):
        for d_band in range(n_band):
            for d_ga in range(n_ga):
                if (d_image, d_band, d_ga) != (0, 0, 0):
                    there = (
                        lax.rem(image + d_image, n_image), lax.rem(band + d_band, n_band), lax.rem(ga + d_ga, n_ga)
                    )
                    pl.semaphore_signal(barrier, inc=1, device_id=there, device_id_type=MESH)

    for c in range(2, CHUNKS):
        start_other(c)
    g_copy.start()
    own_copies = wave_copies(raw_own, side, 0, tiles, own_sem)
    for copy in own_copies:
        copy.start()
    ff_copy.start()

    for copy in small:
        copy.wait()
    for c in range(3):
        for j in range(n_groups):
            pos_wide[c, 8 * j : 8 * j + 8, :] = jnp.broadcast_to(column(pos[0, c : c + 1, :], 8 * j, 8), (8, LANE))
    for s in range(species):
        alive = (iota((slots, LANE), 0) < count[s]).astype(F32)
        live[s] = alive
        strength[s] = alive * column(coup[s : s + 1, :], 0, slots)
    lanes = iota((1, LANE), 1)
    here = lax.rem(lanes // bands, 2) == side
    occ_part[...] = jnp.broadcast_to(jnp.where(here, jnp.concatenate([occ[...]] * (LANE // bands), axis=1), 0.0), (8, LANE))

    def wave_push(c):
        at = pl.ds(c * step_tiles, step_tiles)
        return pltpu.make_async_remote_copy(
            src_ref=w_send.at[:, at], dst_ref=w_all.at[side, :, at],
            send_sem=w_send_sem.at[c], recv_sem=w_recv_sem.at[c],
            device_id={"band": peer}, device_id_type=MESH,
        )

    def wave_arrival(c):
        at = pl.ds(c * step_tiles, step_tiles)
        return pltpu.make_async_remote_copy(
            src_ref=w_send.at[:, at], dst_ref=w_all.at[1 - side, :, at],
            send_sem=w_send_sem.at[c], recv_sem=w_recv_sem.at[c],
            device_id={"band": peer}, device_id_type=MESH,
        )

    occ_push = pltpu.make_async_remote_copy(
        src_ref=occ_part, dst_ref=occ_peer, send_sem=occ_sem.at[0], recv_sem=occ_sem.at[1],
        device_id={"band": peer}, device_id_type=MESH,
    )

    def widen_other(c):
        def one(t, carry):
            at = c * step_tiles + t
            for b in range(blocks):
                w_send[b, at] = raw_other[b, at].astype(F32)
            return carry

        lax.fori_loop(0, step_tiles, one, 0, unroll=8)

    for c in range(CHUNKS):
        for copy in wave_copies(raw_other, 1 - side, c, step_tiles, other_sem.at[c]):
            copy.wait()
        widen_other(c)
        if c == 0:
            pl.semaphore_wait(barrier, 3 * group - 1)
        wave_push(c).start()
    occ_push.start()

    for copy in own_copies:
        copy.wait()

    def widen_own(t, carry):
        for b in range(blocks):
            w_all[side, b, t] = raw_own[b, t].astype(F32)
        return carry

    lax.fori_loop(0, tiles, widen_own, 0, unroll=8)
    g_copy.wait()
    ff_copy.wait()

    def g_rows(at):
        return [jnp.broadcast_to(g[c : c + 1, at], (8, WIDE)) for c in range(3)]

    def doubled(x):
        return jnp.concatenate([x] * (WIDE // LANE), axis=1)

    def prepare(k, trig, rad):
        at = pl.ds(pl.multiple_of(k * WIDE, WIDE), WIDE)
        for s in range(species):
            rad[s] = ff[s, :, at] * doubled(live[s])
        gs = g_rows(at)
        for j in range(n_groups):
            rows = slice(8 * j, 8 * j + 8)
            phases = doubled(pos_wide[0, rows, :]) * gs[0]
            phases = phases + doubled(pos_wide[1, rows, :]) * gs[1]
            phases = phases + doubled(pos_wide[2, rows, :]) * gs[2]
            cosine, minus_sine = cos_and_minus_sin(phases)
            trig[j, 0] = cosine
            trig[j, 1] = minus_sine

    def stage(k):
        at = pl.ds(pl.multiple_of(k * WIDE, WIDE), WIDE)
        gs = g_rows(at)

        def rows(uv):
            pieces = []
            for s in range(2):
                for b in range(blocks):
                    pieces.append(jnp.concatenate(
                        [w_all[s, b, 2 * k + t, pl.ds(uv, 8, stride=2), :] for t in range(WIDE // LANE)], axis=1))
            return pieces

        u, v = rows(0), rows(1)
        real = list(u)
        imag = list(v)
        for c in range(3):
            minus = -gs[c]
            real += [minus * x for x in v]
            imag += [gs[c] * x for x in u]
        pltpu.matmul_push_rhs(jnp.concatenate(real, axis=0).astype(BF16), 0, 0, transpose=True)
        pltpu.matmul_push_rhs(jnp.concatenate(imag, axis=0).astype(BF16), 0, 1, transpose=True)

    def multiply(trig, rad, accs, j):
        radial = [rad[spec[8 * j + i]] for i in range(8)]
        for q in range(2):
            lhs = jnp.concatenate([radial[i] * trig[j, q, i : i + 1, :] for i in range(8)], axis=0).astype(BF16)
            pltpu.matmul_acc_lhs(accs[q][j], lhs, load_staged_rhs=0 if j == 0 else None)

    def with_accumulators(*refs):
        accs = (refs[:n_groups], refs[n_groups:])
        for ref in refs:
            pltpu.matmul_pop(ref)

        def wide_tile(k, now, later):
            after = jnp.minimum(k + 1, n_wide - 1)
            multiply(*now, accs, 0)
            stage(after)
            prepare(after, *later)
            for j in range(1, n_groups):
                multiply(*now, accs, j)

        wave_arrival(0).wait_recv()
        prepare(0, trig_a, rad_a)
        stage(0)
        per_chunk = n_wide // CHUNKS

        def pair(i, carry):
            k = 2 * i

            @pl.when((lax.rem(k + 2, per_chunk) == 0) & (k + 2 < n_wide))
            def _():
                wave_arrival((k + 2) // per_chunk).wait_recv()

            wide_tile(k, (trig_a, rad_a), (trig_b, rad_b))
            wide_tile(k + 1, (trig_b, rad_b), (trig_a, rad_a))
            return carry

        lax.fori_loop(0, n_wide // 2, pair, 0)
        for j in range(n_groups):
            sums = 2.0 * (pltpu.matmul_pop(accs[0][j]) + pltpu.matmul_pop(accs[1][j]))
            for i in range(8 // own_atoms):
                part[j * (8 // own_atoms) + i] = sums[i * own_rows : (i + 1) * own_rows]
        zeros = jnp.zeros((8 * slots, WIDE), BF16)
        for q in range(2):
            pltpu.matmul_acc_lhs(accs[q][0], zeros, load_staged_rhs=0)
            pltpu.matmul_pop(accs[q][0])

    pl.run_scoped(
        with_accumulators,
        *[pltpu.ACC(q)((8 * slots, WIDE), F32) for q in range(2) for _ in range(n_groups)],
    )

    def pair_push(q):
        return pltpu.make_async_remote_copy(
            src_ref=part.at[(1 - side) * n_ga + q], dst_ref=part_peer.at[q],
            send_sem=part_sems.at[0, q], recv_sem=part_sems.at[1, q],
            device_id={"band": peer}, device_id_type=MESH,
        )

    def z_push(d):
        return pltpu.make_async_remote_copy(
            src_ref=z_send.at[d - 1], dst_ref=z_recv.at[d - 1],
            send_sem=z_sems.at[0, d - 1], recv_sem=z_sems.at[1, d - 1],
            device_id={"ga": lax.rem(ga + d, n_ga)}, device_id_type=MESH,
        )

    order = list(range(1, n_ga)) + [0]
    for d in order:
        pair_push(lax.rem(ga + d, n_ga)).start()
    for d in order[:-1]:
        q = lax.rem(ga + d, n_ga)
        pair_push(q).wait_recv()
        z_send[d - 1] = part[side * n_ga + q] + part_peer[q]
        z_push(d).start()
    pair_push(ga).wait_recv()
    occ_push.wait()
    weights = occ_part[0:1, :] + occ_peer[0:1, :]
    sums = part[side * n_ga + ga] + part_peer[ga]
    for d in range(1, n_ga):
        z_push(d).wait_recv()
        sums = sums + z_recv[d - 1]

    owner = side * n_ga + ga
    first = owner * own_atoms
    low = iota((slots, LANE), 1) < LANE // 2
    rows_0, rows_1 = [], []
    for i in range(own_atoms):
        rows = slice(i * slots, (i + 1) * slots)
        left, right = sums[rows, :LANE], sums[rows, LANE:]
        becp = jnp.where(low, left, pltpu.roll(left, LANE // 2, 1))
        weighted = becp * weights * strength[spec[first + i]]
        rows_0.append(jnp.sum(weighted * left, axis=0, keepdims=True))
        rows_1.append(jnp.sum(weighted * right, axis=0, keepdims=True))
    rows_0, rows_1 = jnp.concatenate(rows_0, axis=0), jnp.concatenate(rows_1, axis=0)
    low = iota((own_atoms, LANE), 1) < LANE // 2
    cols = [
        jnp.sum(jnp.where(low == is_low, x, 0.0), axis=1, keepdims=True)
        for x, is_low in ((rows_0, True), (rows_0, False), (rows_1, True), (rows_1, False))
    ]
    energy_part = jnp.broadcast_to(jnp.sum(cols[0], axis=0, keepdims=True), (1, LANE))
    force_part = [-2.0 * row_of(col, first) for col in cols[1:]]

    def padded(x):
        return jnp.concatenate([x, jnp.zeros((x.shape[0], LANE - x.shape[1]), F32)], axis=1)

    rest = jnp.full((1, LANE), erest[0], F32)
    here_pos = padded(pos[0])
    message = jnp.concatenate([energy_part] + force_part + [rest, here_pos], axis=0)
    msg[...] = message
    slot = band * n_ga + ga
    msgs[1, slot] = message

    pushes = []
    count_pushes = 0
    for place, d_image in ((1, 0), (0, 1), (2, n_image - 1)):
        for d_band in range(n_band):
            for d_ga in range(n_ga):
                if (d_image, d_band, d_ga) != (0, 0, 0):
                    there = (
                        lax.rem(image + d_image, n_image), lax.rem(band + d_band, n_band), lax.rem(ga + d_ga, n_ga)
                    )
                    push = pltpu.make_async_remote_copy(
                        src_ref=msg, dst_ref=msgs.at[place, slot],
                        send_sem=msg_send_sem.at[count_pushes], recv_sem=msg_recv_sem.at[place, slot],
                        device_id=there, device_id_type=MESH,
                    )
                    push.start()
                    pushes.append(push)
                    count_pushes += 1
    for place, d_image in ((1, 0), (0, 1), (2, n_image - 1)):
        for d_band in range(n_band):
            for d_ga in range(n_ga):
                if (d_image, d_band, d_ga) != (0, 0, 0):
                    sender = lax.rem(band + d_band, n_band) * n_ga + lax.rem(ga + d_ga, n_ga)
                    pltpu.make_async_remote_copy(
                        src_ref=msg, dst_ref=msgs.at[place, sender],
                        send_sem=msg_send_sem.at[0], recv_sem=msg_recv_sem.at[place, sender],
                        device_id=(image, peer, ga), device_id_type=MESH,
                    ).wait_recv()

    def gathered(place):
        out = msgs[place, 0]
        first_msg = out
        for s in range(1, group):
            out = out + msgs[place, s]
        return first_msg[4:5, 0:1] + out[0:1, 0:1], out[1:4, :], first_msg[5:8, :]

    energy, force_nl, _ = gathered(1)
    prev_energy, _, prev_pos = gathered(0)
    next_energy, _, next_pos = gathered(2)
    ends = [padded(endp[s]) for s in range(2)]
    at_start, at_end = image == 0, image == n_image - 1
    prev_pos = jnp.where(jnp.full((3, LANE), at_start), ends[0], prev_pos)
    next_pos = jnp.where(jnp.full((3, LANE), at_end), ends[1], next_pos)
    prev_energy = jnp.where(jnp.full((1, 1), at_start), jnp.full((1, 1), ende[0], F32), prev_energy)
    next_energy = jnp.where(jnp.full((1, 1), at_end), jnp.full((1, 1), ende[1], F32), next_energy)
    force = padded(frest[0]) + force_nl

    to_next = next_pos - here_pos
    from_prev = here_pos - prev_pos
    rise_next = jnp.abs(next_energy - energy)
    rise_prev = jnp.abs(prev_energy - energy)
    larger = jnp.maximum(rise_next, rise_prev)
    smaller = jnp.minimum(rise_next, rise_prev)
    rising = next_energy > prev_energy
    weight_next = 1.0 + jnp.where(rising, larger, smaller)
    weight_prev = 1.0 + jnp.where(rising, smaller, larger)
    stiff_next = SPRING * (1.0 + 1.0 / (1.0 + jnp.exp(-0.5 * (next_energy + energy))))
    stiff_prev = SPRING * (1.0 + 1.0 / (1.0 + jnp.exp(-0.5 * (prev_energy + energy))))
    length_next = jnp.sqrt(total(to_next * to_next) + 1.0)
    length_prev = jnp.sqrt(total(from_prev * from_prev) + 1.0)
    upwind = weight_next * to_next + weight_prev * from_prev
    forward = to_next / length_next
    backward = from_prev / length_prev
    rule = jnp.full((3, LANE), kind[0], jnp.int32)
    tangent = jnp.where(
        rule == 0, upwind, jnp.where(rule == 1, forward + backward, jnp.where(rule == 2, forward, backward))
    )
    unit = tangent / jnp.sqrt(total(tangent * tangent) + 1.0)
    along = total(force * unit)
    climbing = force - 2.0 * along * unit
    regular = force - along * unit + (stiff_next * length_next - stiff_prev * length_prev) * unit
    is_climb = jnp.full((3, LANE), climb[0], jnp.int32) == image
    result = jnp.where(is_climb, climbing, regular)
    force_out[0] = result[:, :atoms]
    energy_out[0] = jnp.sum(energy)

    for c in range(CHUNKS):
        wave_push(c).wait_send()
    for d in order:
        pair_push(lax.rem(ga + d, n_ga)).wait_send()
    for d in range(1, n_ga):
        z_push(d).wait_send()
    for push in pushes:
        push.wait_send()


def per_device(
    wave_coeffs, occupation, form_factor, g_vectors, species, proj_count, coupling, positions, energy_rest,
    force_rest, end_positions, end_energy, climb_index, tangent_kind,
):
    _, bands, _, length = wave_coeffs.shape
    kinds, slots, _ = form_factor.shape
    atoms = species.shape[0]
    n_band, n_ga = lax.axis_size("band"), lax.axis_size("ga")
    waves = wave_coeffs[0].reshape(bands, 2, length // LANE, LANE).transpose(0, 2, 1, 3)
    blocks = bands // 8
    tiles = length // (2 * LANE)
    half_len = length // 2
    owners = 2 * n_ga
    own_rows = atoms * slots // owners
    group = n_band * n_ga
    args = (
        waves, occupation, form_factor, g_vectors, species, proj_count, coupling, positions, energy_rest,
        force_rest, end_positions, end_energy, climb_index, tangent_kind,
    )
    vmem, smem, dma = pltpu.VMEM, pltpu.SMEM, pltpu.SemaphoreType.DMA
    return pl.pallas_call(
        kernel,
        in_specs=[pl.BlockSpec(memory_space=pl.ANY)] * len(args),
        out_specs=[pl.BlockSpec(memory_space=pltpu.VMEM), pl.BlockSpec(memory_space=pltpu.SMEM)],
        out_shape=[jax.ShapeDtypeStruct(force_rest.shape, F32), jax.ShapeDtypeStruct(energy_rest.shape, F32)],
        scratch_shapes=[
            vmem((blocks, tiles, 16, LANE), BF16),
            vmem((blocks, tiles, 16, LANE), BF16),
            vmem((blocks, tiles, 16, LANE), F32),
            vmem((2, blocks, tiles, 16, LANE), F32),
            vmem((kinds, slots, half_len), F32),
            vmem((3, half_len), F32),
            vmem(positions.shape, F32),
            vmem(coupling.shape, F32),
            vmem(occupation.shape, F32),
            smem(energy_rest.shape, F32),
            vmem(force_rest.shape, F32),
            vmem(end_positions.shape, F32),
            smem(end_energy.shape, F32),
            smem(species.shape, jnp.int32),
            smem(proj_count.shape, jnp.int32),
            smem(climb_index.shape, jnp.int32),
            smem(tangent_kind.shape, jnp.int32),
            vmem((3, atoms, LANE), F32),
            vmem((kinds, slots, LANE), F32),
            vmem((kinds, slots, LANE), F32),
            vmem((8, LANE), F32),
            vmem((8, LANE), F32),
            vmem((atoms // 8, 2, 8, WIDE), F32),
            vmem((atoms // 8, 2, 8, WIDE), F32),
            vmem((kinds, slots, WIDE), F32),
            vmem((kinds, slots, WIDE), F32),
            vmem((owners, own_rows, WIDE), F32),
            vmem((n_ga, own_rows, WIDE), F32),
            vmem((n_ga - 1, own_rows, WIDE), F32),
            vmem((n_ga - 1, own_rows, WIDE), F32),
            vmem((8, LANE), F32),
            vmem((3, group, 8, LANE), F32),
            dma((11,)),
            dma((CHUNKS,)),
            dma(()),
            dma(()),
            dma(()),
            dma((CHUNKS,)),
            dma((CHUNKS,)),
            dma((2,)),
            dma((2, n_ga)),
            dma((2, n_ga - 1)),
            dma((3 * group - 1,)),
            dma((3, group)),
        ],
        compiler_params=pltpu.CompilerParams(
            collective_id=0, has_side_effects=True, vmem_limit_bytes=60 * 1024 * 1024
        ),
    )(*args)


def solution(mesh):
    in_specs = (
        P("image", "band", None, "ga"),
        P("image", "band"),
        P(None, None, "ga"),
        P(None, "ga"),
        P(),
        P(),
        P(),
        P("image", None, None),
        P("image"),
        P("image", None, None),
        P(),
        P(),
        P(),
        P("image"),
    )
    out_specs = (P("image", None, None), P("image"))

    def run(*args):
        with jax.sharding.use_abstract_mesh(mesh.abstract_mesh):
            return jax.shard_map(
                per_device, mesh=mesh, in_specs=in_specs, out_specs=out_specs, check_vma=False
            )(*args)

    return run
```

time: 185 us -> 62.3 us (0.34)
  Pallas kernels: 94.8 us -> 52.5 us
  waiting for transfers between devices: 20.1 us -> 0 us
  between operations: 23.4 us -> 4.33 us
  blocking collectives: 14.3 us -> 0 us
  starting transfers between devices: 12.8 us -> 0 us
  local copies, waits for them, and re-layouts: 13.6 us -> 4.99 us
  other arithmetic: 5.94 us -> 0 us
    pallas_call x1, Pallas kernels: 94.8 us -> 52.5 us  [per_device(): pl.pallas_call(kernel, in_specs=[pl.BlockSpec(memory_space=pl.ANY)] * len...]
    reduce_scatter x1 -> x0, waiting for transfers between devices: 17.2 us -> none  [per_device(): proj_sums = lax.psum_scatter(sums, 'ga', scatter_dimension=0, tiled=True)]
    psum x1 -> x0, blocking collectives: 14.3 us -> none  [per_device(): force_nl, energy_nl = lax.psum((force_full, energy_part), ('band', 'ga'))]
    ppermute x4 -> x0, starting transfers between devices: 12.7 us -> none  [passed_along(): return lax.ppermute(array, axis, pairs)]
    transpose x1 -> x0, local copies, waits for them, and re-layouts: 11.3 us -> none  [projector_sums(): w = jnp.swapaxes(waves, 0, 1).reshape(2 * bands, length)]
    reduce_sum x6 -> x0, other arithmetic: 3.93 us -> none  [the longest x1 1.21 us: nonlocal_terms(): per_row = jnp.sum(weighted * slope, axis=1).reshape(atom_count, PMAX)]
    unnamed x17 -> x3, local copies, waits for them, and re-layouts: 0.74 us -> 3.77 us
    ppermute x4 -> x0, waiting for transfers between devices: 2.93 us -> none  [passed_along(): return lax.ppermute(array, axis, pairs)]
  transfers between devices with their start and end apart: 5 -> 0, of which waited for: 2 -> 0; matrix products, arithmetic and copies ran while one was open for 8% -> 0% of each run, Pallas kernels for 51% -> 0%
where the time goes in v1:
time: 62.3 us; the launch traced here: 61.8 us
  Pallas kernels  52.5 us (84%)
  local copies, waits for them, and re-layouts  4.99 us (8%)
  between operations  4.33 us (7%)
    pallas_call x1, Pallas kernels, per_device(): pl.pallas_call(kernel, in_specs=[pl.BlockSpec(memory_space=pl.ANY)] * len...  52.5 us
    unnamed x3, local copies, waits for them, and re-layouts  3.77 us

profile of v1, /device:TPU:0, one launch (start us, length us, event | category | flops | bytes accessed | tf_op | source)
XLA Modules:
  0.0 61.8 jit_solution(13656400104342537182)
XLA Ops:
  2.6 1.2 %copy.16.pos_hbm = f32[1,3,64]{2,1,0:T(4,128)} copy(f32[1,3,64]{2,0,1:T(1,128)} %param.21) | data formatting | bytes 1536 | tf_op args[7]
  3.8 1.3 %copy.17.frest_hbm = f32[1,3,64]{2,1,0:T(4,128)} copy(f32[1,3,64]{2,0,1:T(1,128)} %param.23) | data formatting | bytes 1536 | tf_op args[9]
  5.1 1.3 %copy.18.endp_hbm = f32[2,3,64]{2,1,0:T(4,128)} copy(f32[2,3,64]{2,0,1:T(2,128)} %param.24) | data formatting | bytes 3072 | tf_op args[10]
  6.3 52.5 %shard_map.149 = (f32[1,3,64]{2,1,0:T(4,128)}, f32[1]{0:T(128)}) custom-call(bf16[32,512,2,128]{3,2,1,0:T(2,128)(2,1)} %bitcast.3, f32[1,32]{1,0:T(1,128)} %occ_hbm.1, f32[4,8,65536]{2,1,0:T(8,128)} %ff_hbm.1, f32[3,65536]{1,0:T(4,128)} %g_hbm.1, s32[64]{0:T(128)} %spec_hbm.1, s32[4]{0:T(128)} %count_hbm.1, f32[4,8]{1,0:T(4,128)} %coup_hbm.1, ...), custom_call_target="tpu_custom_call" | custom-call | tf_op jit(solution)/shard_map/pallas_call | solution.py:455
  58.9 1.2 %copy.19 = f32[1,3,64]{2,0,1:T(1,128)} copy(f32[1,3,64]{2,1,0:T(4,128)} %get-tuple-element.2) | data formatting | bytes 1536 | tf_op jit(solution)/shard_map/pallas_call | solution.py:455

commit v2 on v1

--- a/solution.py
+++ b/solution.py
@@ -8,10 +8,8 @@
 from jax.sharding import PartitionSpec as P
 
 SPRING = 5.0
-SIN_HALF = (0.7071067780965931, -0.02946276693049568, 0.00036827213876565137, -2.1885830267998076e-06, 7.194201360627222e-09)
-COS_HALF = (-1.4142134949348355, 0.17677635430234293, -0.003682571658574129, 3.061195661905538e-05, -1.2786908538293617e-07)
-TURN_HIGH = 6.28125
-TURN_LOW = 0.001935307179586232
+SIN_HALF = (4.442882834139934, -7.308241153900935, 3.6062889473068847, -0.8457635292167789, 0.10920561914186756)
+COS_HALF = (-1.414213496558818, 6.978850987079544, -5.739461141869309, 1.8835627683448501, -0.31069768559559485)
 ROUNDER = 12582912.0
 LANE = 128
 WIDE = 256
@@ -29,8 +27,8 @@
 
 
 def cos_and_minus_sin(phases):
-    turns = (phases * 0.15915494309189535 + ROUNDER) - ROUNDER
-    r = (phases - turns * TURN_HIGH) - turns * TURN_LOW
+    turns = phases * 0.15915494309189535
+    r = turns - ((turns + ROUNDER) - ROUNDER)
     z = r * r
     half_sin = r * horner(SIN_HALF, z)
     return (1.0 - half_sin * half_sin, half_sin * horner(COS_HALF, z))
@@ -62,7 +60,7 @@
     force_out, energy_out,
     raw_other, raw_own, w_send, w_all, ff, g, pos, coup, occ, erest, frest, endp, ende,
     spec, count, climb, kind,
-    pos_wide, live, strength, occ_part, occ_peer, trig_a, trig_b, rad_a, rad_b,
+    pos_wide, live, strength, occ_part, occ_peer, rad_a, rad_b, trig_a, trig_b,
     part, part_peer, z_send, z_recv, msg, msgs,
     small_sem, other_sem, own_sem, ff_sem, g_sem, w_send_sem, w_recv_sem, occ_sem,
     part_sems, z_sems, msg_send_sem, msg_recv_sem,
@@ -79,9 +77,10 @@
     half_len = ff.shape[2]
     n_wide = half_len // WIDE
     step_tiles = tiles // CHUNKS
-    owners = part.shape[0]
-    own_atoms = atoms // owners
-    own_rows = part.shape[1]
+    n_own = z_send.shape[0]
+    own_rows = z_send.shape[1]
+    own_atoms = own_rows // slots
+    first_own = (n_ga - n_own) // 2
     n_groups = atoms // 8
 
     small = [
@@ -108,11 +107,6 @@
     mine = pl.ds(pl.multiple_of(side * half_len, WIDE), half_len)
     ff_copy = pltpu.make_async_copy(ff_hbm.at[:, :, mine], ff, ff_sem)
     g_copy = pltpu.make_async_copy(g_hbm.at[:, mine], g, g_sem)
-    start_other(0)
-    for copy in small:
-        copy.start()
-    start_other(1)
-
     barrier = pltpu.get_barrier_semaphore()
     for d_image in (0, 1, n_image - 1):
         for d_band in range(n_band):
@@ -123,6 +117,11 @@
                     )
                     pl.semaphore_signal(barrier, inc=1, device_id=there, device_id_type=MESH)
 
+    start_other(0)
+    for copy in small:
+        copy.start()
+    start_other(1)
+
     for c in range(2, CHUNKS):
         start_other(c)
     g_copy.start()
@@ -135,7 +134,7 @@
         copy.wait()
     for c in range(3):
         for j in range(n_groups):
-            pos_wide[c, 8 * j : 8 * j + 8, :] = jnp.broadcast_to(column(pos[0, c : c + 1, :], 8 * j, 8), (8, LANE))
+            pos_wide[c, 8 * j : 8 * j + 8, :] = jnp.broadcast_to(column(pos[c], 8 * j, 8), (8, LANE))
     for s in range(species):
         alive = (iota((slots, LANE), 0) < count[s]).astype(F32)
         live[s] = alive
@@ -196,24 +195,26 @@
     ff_copy.wait()
 
     def g_rows(at):
-        return [jnp.broadcast_to(g[c : c + 1, at], (8, WIDE)) for c in range(3)]
-
-    def doubled(x):
-        return jnp.concatenate([x] * (WIDE // LANE), axis=1)
-
-    def prepare(k, trig, rad):
-        at = pl.ds(pl.multiple_of(k * WIDE, WIDE), WIDE)
-        for s in range(species):
-            rad[s] = ff[s, :, at] * doubled(live[s])
-        gs = g_rows(at)
-        for j in range(n_groups):
-            rows = slice(8 * j, 8 * j + 8)
-            phases = doubled(pos_wide[0, rows, :]) * gs[0]
-            phases = phases + doubled(pos_wide[1, rows, :]) * gs[1]
-            phases = phases + doubled(pos_wide[2, rows, :]) * gs[2]
+        return [jnp.broadcast_to(g[c : c + 1, at], (8, at.size)) for c in range(3)]
+
+    def span(k, t):
+        return pl.ds(pl.multiple_of(k * WIDE + t * LANE, LANE), LANE)
+
+    def radial(k, rad):
+        for t in range(WIDE // LANE):
+            for s in range(species):
+                rad[s, t] = ff[s, :, span(k, t)] * live[s]
+
+    def waves_of_atoms(k, trig, j):
+        rows = slice(8 * j, 8 * j + 8)
+        for t in range(WIDE // LANE):
+            gs = g_rows(span(k, t))
+            phases = pos_wide[0, rows, :] * gs[0]
+            phases = phases + pos_wide[1, rows, :] * gs[1]
+            phases = phases + pos_wide[2, rows, :] * gs[2]
             cosine, minus_sine = cos_and_minus_sin(phases)
-            trig[j, 0] = cosine
-            trig[j, 1] = minus_sine
+            trig[j, 0, t] = cosine
+            trig[j, 1, t] = minus_sine
 
     def stage(k):
         at = pl.ds(pl.multiple_of(k * WIDE, WIDE), WIDE)
@@ -234,14 +235,22 @@
             minus = -gs[c]
             real += [minus * x for x in v]
             imag += [gs[c] * x for x in u]
-        pltpu.matmul_push_rhs(jnp.concatenate(real, axis=0).astype(BF16), 0, 0, transpose=True)
-        pltpu.matmul_push_rhs(jnp.concatenate(imag, axis=0).astype(BF16), 0, 1, transpose=True)
-
-    def multiply(trig, rad, accs, j):
-        radial = [rad[spec[8 * j + i]] for i in range(8)]
+        pltpu.matmul_push_rhs(jnp.concatenate(real, axis=0), 0, 0, transpose=True)
+        pltpu.matmul_push_rhs(jnp.concatenate(imag, axis=0), 0, 1, transpose=True)
+
+    def projector(rad, trig, j):
+        pieces = ([], [])
+        for i in range(8):
+            kind_of = spec[8 * j + i]
+            factors = [rad[kind_of, t] for t in range(WIDE // LANE)]
+            for q in range(2):
+                pieces[q].append(jnp.concatenate(
+                    [factors[t] * trig[j, q, t, i : i + 1, :] for t in range(WIDE // LANE)], axis=1))
+        return [jnp.concatenate(pieces[q], axis=0) for q in range(2)]
+
+    def multiply(lhs, accs, j):
         for q in range(2):
-            lhs = jnp.concatenate([radial[i] * trig[j, q, i : i + 1, :] for i in range(8)], axis=0).astype(BF16)
-            pltpu.matmul_acc_lhs(accs[q][j], lhs, load_staged_rhs=0 if j == 0 else None)
+            pltpu.matmul_acc_lhs(accs[q][j], lhs[q], load_staged_rhs=0 if j == 0 else None)
 
     def with_accumulators(*refs):
         accs = (refs[:n_groups], refs[n_groups:])
@@ -249,15 +258,20 @@
             pltpu.matmul_pop(ref)
 
         def wide_tile(k, now, later):
-            after = jnp.minimum(k + 1, n_wide - 1)
-            multiply(*now, accs, 0)
-            stage(after)
-            prepare(after, *later)
-            for j in range(1, n_groups):
-                multiply(*now, accs, j)
-
+            after, second = jnp.minimum(k + 1, n_wide - 1), jnp.minimum(k + 2, n_wide - 1)
+            rad, trig = now
+            radial(after, later[0])
+            for j in range(n_groups):
+                multiply(projector(rad, trig, j), accs, j)
+                if j == 0:
+                    stage(after)
+                waves_of_atoms(second, trig, j)
+
+        radial(0, rad_a)
+        for j in range(n_groups):
+            waves_of_atoms(0, trig_a, j)
+            waves_of_atoms(1, trig_b, j)
         wave_arrival(0).wait_recv()
-        prepare(0, trig_a, rad_a)
         stage(0)
         per_chunk = n_wide // CHUNKS
 
@@ -268,16 +282,15 @@
             def _():
                 wave_arrival((k + 2) // per_chunk).wait_recv()
 
-            wide_tile(k, (trig_a, rad_a), (trig_b, rad_b))
-            wide_tile(k + 1, (trig_b, rad_b), (trig_a, rad_a))
+            wide_tile(k, (rad_a, trig_a), (rad_b, trig_b))
+            wide_tile(k + 1, (rad_b, trig_b), (rad_a, trig_a))
             return carry
 
         lax.fori_loop(0, n_wide // 2, pair, 0)
         for j in range(n_groups):
             sums = 2.0 * (pltpu.matmul_pop(accs[0][j]) + pltpu.matmul_pop(accs[1][j]))
-            for i in range(8 // own_atoms):
-                part[j * (8 // own_atoms) + i] = sums[i * own_rows : (i + 1) * own_rows]
-        zeros = jnp.zeros((8 * slots, WIDE), BF16)
+            part[j * 8 * slots : (j + 1) * 8 * slots, :] = sums
+        zeros = jnp.zeros((8 * slots, WIDE), F32)
         for q in range(2):
             pltpu.matmul_acc_lhs(accs[q][0], zeros, load_staged_rhs=0)
             pltpu.matmul_pop(accs[q][0])
@@ -287,111 +300,138 @@
         *[pltpu.ACC(q)((8 * slots, WIDE), F32) for q in range(2) for _ in range(n_groups)],
     )
 
+    def block(of_side, q):
+        return pl.ds(pl.multiple_of((of_side * n_own + q) * own_rows, own_rows), own_rows)
+
     def pair_push(q):
         return pltpu.make_async_remote_copy(
-            src_ref=part.at[(1 - side) * n_ga + q], dst_ref=part_peer.at[q],
+            src_ref=part.at[block(1 - side, q)], dst_ref=part_peer.at[q],
             send_sem=part_sems.at[0, q], recv_sem=part_sems.at[1, q],
             device_id={"band": peer}, device_id_type=MESH,
         )
 
-    def z_push(d):
+    def z_push(q):
+        there = first_own + q
         return pltpu.make_async_remote_copy(
-            src_ref=z_send.at[d - 1], dst_ref=z_recv.at[d - 1],
-            send_sem=z_sems.at[0, d - 1], recv_sem=z_sems.at[1, d - 1],
-            device_id={"ga": lax.rem(ga + d, n_ga)}, device_id_type=MESH,
+            src_ref=z_send.at[q], dst_ref=z_recv.at[ga],
+            send_sem=z_sems.at[0, q], recv_sem=z_sems.at[1, ga],
+            device_id={"ga": there}, device_id_type=MESH,
         )
 
-    order = list(range(1, n_ga)) + [0]
-    for d in order:
-        pair_push(lax.rem(ga + d, n_ga)).start()
-    for d in order[:-1]:
-        q = lax.rem(ga + d, n_ga)
+    def z_arrival(sender):
+        return pltpu.make_async_remote_copy(
+            src_ref=z_send.at[0], dst_ref=z_recv.at[sender],
+            send_sem=z_sems.at[0, 0], recv_sem=z_sems.at[1, sender],
+            device_id={"band": peer}, device_id_type=MESH,
+        )
+
+    in_upper = (ga >= first_own + n_own // 2).astype(jnp.int32)
+    order = [q * in_upper + (n_own - 1 - q) * (1 - in_upper) for q in range(n_own)]
+    is_owner = (ga >= first_own) & (ga < first_own + n_own)
+    for q in order:
+        pair_push(q).start()
+    for q in order:
         pair_push(q).wait_recv()
-        z_send[d - 1] = part[side * n_ga + q] + part_peer[q]
-        z_push(d).start()
-    pair_push(ga).wait_recv()
+        z_send[q] = part[block(side, q), :] + part_peer[q]
+
+        @pl.when(ga != first_own + q)
+        def _():
+            z_push(q).start()
+
     occ_push.wait()
     weights = occ_part[0:1, :] + occ_peer[0:1, :]
-    sums = part[side * n_ga + ga] + part_peer[ga]
-    for d in range(1, n_ga):
-        z_push(d).wait_recv()
-        sums = sums + z_recv[d - 1]
-
-    owner = side * n_ga + ga
-    first = owner * own_atoms
-    low = iota((slots, LANE), 1) < LANE // 2
-    rows_0, rows_1 = [], []
-    for i in range(own_atoms):
-        rows = slice(i * slots, (i + 1) * slots)
-        left, right = sums[rows, :LANE], sums[rows, LANE:]
-        becp = jnp.where(low, left, pltpu.roll(left, LANE // 2, 1))
-        weighted = becp * weights * strength[spec[first + i]]
-        rows_0.append(jnp.sum(weighted * left, axis=0, keepdims=True))
-        rows_1.append(jnp.sum(weighted * right, axis=0, keepdims=True))
-    rows_0, rows_1 = jnp.concatenate(rows_0, axis=0), jnp.concatenate(rows_1, axis=0)
-    low = iota((own_atoms, LANE), 1) < LANE // 2
-    cols = [
-        jnp.sum(jnp.where(low == is_low, x, 0.0), axis=1, keepdims=True)
-        for x, is_low in ((rows_0, True), (rows_0, False), (rows_1, True), (rows_1, False))
-    ]
-    energy_part = jnp.broadcast_to(jnp.sum(cols[0], axis=0, keepdims=True), (1, LANE))
-    force_part = [-2.0 * row_of(col, first) for col in cols[1:]]
+    place_own = jnp.clip(ga - first_own, 0, n_own - 1)
+    group_own = n_band * n_own
+    slot = band * n_own + place_own
+    here_pos = jnp.concatenate([pos[:, 0, :], jnp.zeros((3, LANE - atoms), F32)], axis=1)
+
+    def own_message():
+        for d in range(1, n_ga):
+            z_arrival(lax.rem(ga + d, n_ga)).wait_recv()
+        sums = z_send[place_own]
+        for d in range(1, n_ga):
+            sums = sums + z_recv[lax.rem(ga + d, n_ga)]
+        first = (side * n_own + place_own) * own_atoms
+        low = iota((slots, LANE), 1) < LANE // 2
+        rows_0, rows_1 = [], []
+        for i in range(own_atoms):
+            rows = slice(i * slots, (i + 1) * slots)
+            left, right = sums[rows, :LANE], sums[rows, LANE:]
+            becp = jnp.where(low, left, pltpu.roll(left, LANE // 2, 1))
+            weighted = becp * weights * strength[spec[first + i]]
+            rows_0.append(jnp.sum(weighted * left, axis=0, keepdims=True))
+            rows_1.append(jnp.sum(weighted * right, axis=0, keepdims=True))
+        rows_0, rows_1 = jnp.concatenate(rows_0, axis=0), jnp.concatenate(rows_1, axis=0)
+        low = iota((own_atoms, LANE), 1) < LANE // 2
+        cols = [
+            jnp.sum(jnp.where(low == is_low, x, 0.0), axis=1, keepdims=True)
+            for x, is_low in ((rows_0, True), (rows_0, False), (rows_1, True), (rows_1, False))
+        ]
+        energy_part = jnp.broadcast_to(jnp.sum(cols[0], axis=0, keepdims=True), (1, LANE))
+        force_part = [-2.0 * row_of(col, first) for col in cols[1:]]
+        rest = jnp.full((1, LANE), erest[0], F32)
+        return jnp.concatenate([energy_part] + force_part + [rest, here_pos], axis=0)
 
     def padded(x):
         return jnp.concatenate([x, jnp.zeros((x.shape[0], LANE - x.shape[1]), F32)], axis=1)
 
-    rest = jnp.full((1, LANE), erest[0], F32)
-    here_pos = padded(pos[0])
-    message = jnp.concatenate([energy_part] + force_part + [rest, here_pos], axis=0)
-    msg[...] = message
-    slot = band * n_ga + ga
-    msgs[1, slot] = message
-
-    pushes = []
-    count_pushes = 0
-    for place, d_image in ((1, 0), (0, 1), (2, n_image - 1)):
-        for d_band in range(n_band):
-            for d_ga in range(n_ga):
-                if (d_image, d_band, d_ga) != (0, 0, 0):
-                    there = (
-                        lax.rem(image + d_image, n_image), lax.rem(band + d_band, n_band), lax.rem(ga + d_ga, n_ga)
-                    )
-                    push = pltpu.make_async_remote_copy(
-                        src_ref=msg, dst_ref=msgs.at[place, slot],
-                        send_sem=msg_send_sem.at[count_pushes], recv_sem=msg_recv_sem.at[place, slot],
-                        device_id=there, device_id_type=MESH,
-                    )
-                    push.start()
-                    pushes.append(push)
-                    count_pushes += 1
-    for place, d_image in ((1, 0), (0, 1), (2, n_image - 1)):
-        for d_band in range(n_band):
-            for d_ga in range(n_ga):
-                if (d_image, d_band, d_ga) != (0, 0, 0):
-                    sender = lax.rem(band + d_band, n_band) * n_ga + lax.rem(ga + d_ga, n_ga)
-                    pltpu.make_async_remote_copy(
-                        src_ref=msg, dst_ref=msgs.at[place, sender],
-                        send_sem=msg_send_sem.at[0], recv_sem=msg_recv_sem.at[place, sender],
-                        device_id=(image, peer, ga), device_id_type=MESH,
-                    ).wait_recv()
+    def message_pushes():
+        pushes = []
+        for place, d_image in ((1, 0), (0, 1), (2, n_image - 1)):
+            for d_band in range(n_band):
+                for d_ga in range(n_ga):
+                    if (d_image, d_band, d_ga) != (0, 0, 0):
+                        there = (
+                            lax.rem(image + d_image, n_image), lax.rem(band + d_band, n_band), lax.rem(ga + d_ga, n_ga)
+                        )
+                        pushes.append(pltpu.make_async_remote_copy(
+                            src_ref=msg, dst_ref=msgs.at[place, slot],
+                            send_sem=msg_send_sem.at[len(pushes)], recv_sem=msg_recv_sem.at[place, slot],
+                            device_id=there, device_id_type=MESH,
+                        ))
+        return pushes
+
+    @pl.when(is_owner)
+    def _():
+        message = own_message()
+        msg[...] = message
+        msgs[1, slot] = message
+        for push in message_pushes():
+            push.start()
+
+    for place in (1, 0, 2):
+        for sender in range(group_own):
+            arrival = pltpu.make_async_remote_copy(
+                src_ref=msg, dst_ref=msgs.at[place, sender],
+                send_sem=msg_send_sem.at[0], recv_sem=msg_recv_sem.at[place, sender],
+                device_id=(image, peer, ga), device_id_type=MESH,
+            )
+            if place == 1:
+
+                @pl.when(jnp.logical_not(is_owner & (slot == sender)))
+                def _():
+                    arrival.wait_recv()
+
+            else:
+                arrival.wait_recv()
 
     def gathered(place):
         out = msgs[place, 0]
         first_msg = out
-        for s in range(1, group):
+        for s in range(1, group_own):
             out = out + msgs[place, s]
         return first_msg[4:5, 0:1] + out[0:1, 0:1], out[1:4, :], first_msg[5:8, :]
 
     energy, force_nl, _ = gathered(1)
     prev_energy, _, prev_pos = gathered(0)
     next_energy, _, next_pos = gathered(2)
-    ends = [padded(endp[s]) for s in range(2)]
+    ends = [padded(endp[:, s, :]) for s in range(2)]
     at_start, at_end = image == 0, image == n_image - 1
     prev_pos = jnp.where(jnp.full((3, LANE), at_start), ends[0], prev_pos)
     next_pos = jnp.where(jnp.full((3, LANE), at_end), ends[1], next_pos)
     prev_energy = jnp.where(jnp.full((1, 1), at_start), jnp.full((1, 1), ende[0], F32), prev_energy)
     next_energy = jnp.where(jnp.full((1, 1), at_end), jnp.full((1, 1), ende[1], F32), next_energy)
-    force = padded(frest[0]) + force_nl
+    force = padded(frest[:, 0, :]) + force_nl
 
     to_next = next_pos - here_pos
     from_prev = here_pos - prev_pos
@@ -419,17 +459,23 @@
     regular = force - along * unit + (stiff_next * length_next - stiff_prev * length_prev) * unit
     is_climb = jnp.full((3, LANE), climb[0], jnp.int32) == image
     result = jnp.where(is_climb, climbing, regular)
-    force_out[0] = result[:, :atoms]
-    energy_out[0] = jnp.sum(energy)
+    for c in range(3):
+        force_out[c] = result[c : c + 1, :atoms]
+    energy_out[...] = energy
 
     for c in range(CHUNKS):
         wave_push(c).wait_send()
-    for d in order:
-        pair_push(lax.rem(ga + d, n_ga)).wait_send()
-    for d in range(1, n_ga):
-        z_push(d).wait_send()
-    for push in pushes:
-        push.wait_send()
+    for q in range(n_own):
+        pair_push(q).wait_send()
+
+        @pl.when(ga != first_own + q)
+        def _():
+            z_push(q).wait_send()
+
+    @pl.when(is_owner)
+    def _():
+        for push in message_pushes():
+            push.wait_send()
 
 
 def per_device(
@@ -444,19 +490,20 @@
     blocks = bands // 8
     tiles = length // (2 * LANE)
     half_len = length // 2
-    owners = 2 * n_ga
-    own_rows = atoms * slots // owners
+    n_own = min(n_ga, 2)
+    own_rows = atoms * slots // (2 * n_own)
     group = n_band * n_ga
+    positions, force_rest, end_positions = (x.transpose(1, 0, 2) for x in (positions, force_rest, end_positions))
     args = (
         waves, occupation, form_factor, g_vectors, species, proj_count, coupling, positions, energy_rest,
         force_rest, end_positions, end_energy, climb_index, tangent_kind,
     )
     vmem, smem, dma = pltpu.VMEM, pltpu.SMEM, pltpu.SemaphoreType.DMA
-    return pl.pallas_call(
+    force, energy = pl.pallas_call(
         kernel,
-        in_specs=[pl.BlockSpec(memory_space=pl.ANY)] * len(args),
-        out_specs=[pl.BlockSpec(memory_space=pltpu.VMEM), pl.BlockSpec(memory_space=pltpu.SMEM)],
-        out_shape=[jax.ShapeDtypeStruct(force_rest.shape, F32), jax.ShapeDtypeStruct(energy_rest.shape, F32)],
+        in_specs=[pl.BlockSpec(memory_space=pltpu.HBM)] * len(args),
+        out_specs=[pl.BlockSpec(memory_space=pltpu.VMEM)] * 2,
+        out_shape=[jax.ShapeDtypeStruct(force_rest.shape, F32), jax.ShapeDtypeStruct((1, 1), F32)],
         scratch_shapes=[
             vmem((blocks, tiles, 16, LANE), BF16),
             vmem((blocks, tiles, 16, LANE), BF16),
@@ -480,16 +527,16 @@
             vmem((kinds, slots, LANE), F32),
             vmem((8, LANE), F32),
             vmem((8, LANE), F32),
-            vmem((atoms // 8, 2, 8, WIDE), F32),
-            vmem((atoms // 8, 2, 8, WIDE), F32),
-            vmem((kinds, slots, WIDE), F32),
-            vmem((kinds, slots, WIDE), F32),
-            vmem((owners, own_rows, WIDE), F32),
+            vmem((kinds, 4, 8, LANE), F32),
+            vmem((kinds, 4, 8, LANE), F32),
+            vmem((atoms // 8, 2, WIDE // LANE, 8, LANE), F32),
+            vmem((atoms // 8, 2, WIDE // LANE, 8, LANE), F32),
+            vmem((atoms * slots, WIDE), F32),
+            vmem((n_own, own_rows, WIDE), F32),
+            vmem((n_own, own_rows, WIDE), F32),
             vmem((n_ga, own_rows, WIDE), F32),
-            vmem((n_ga - 1, own_rows, WIDE), F32),
-            vmem((n_ga - 1, own_rows, WIDE), F32),
             vmem((8, LANE), F32),
-            vmem((3, group, 8, LANE), F32),
+            vmem((3, n_band * n_own, 8, LANE), F32),
             dma((11,)),
             dma((CHUNKS,)),
             dma(()),
@@ -498,15 +545,16 @@
             dma((CHUNKS,)),
             dma((CHUNKS,)),
             dma((2,)),
+            dma((2, n_own)),
             dma((2, n_ga)),
-            dma((2, n_ga - 1)),
             dma((3 * group - 1,)),
-            dma((3, group)),
+            dma((3, n_band * n_own)),
         ],
         compiler_params=pltpu.CompilerParams(
             collective_id=0, has_side_effects=True, vmem_limit_bytes=60 * 1024 * 1024
         ),
     )(*args)
+    return force.transpose(1, 0, 2), energy.reshape(1)
 
 
 def solution(mesh):

time: 62.3 us -> 52.7 us (0.85)
  Pallas kernels: 52.5 us -> 47 us
  local copies, waits for them, and re-layouts: 4.99 us -> 1.23 us
    pallas_call x1, Pallas kernels: 52.5 us -> 47 us  [per_device(): pl.pallas_call(kernel, in_specs=[pl.BlockSpec(memory_space=pltpu.HBM)] *...]
    unnamed x3 -> x1, local copies, waits for them, and re-layouts: 3.77 us -> 1.23 us
    pallas_call x1 -> x0, local copies, waits for them, and re-layouts: 1.22 us -> none  [per_device(): pl.pallas_call(kernel, in_specs=[pl.BlockSpec(memory_space=pl.ANY)] * len...]
where the time goes in v2:
time: 52.7 us; the launch traced here: 52.5 us
  Pallas kernels  47 us (89%)
  between operations  4.34 us (8%)
  local copies, waits for them, and re-layouts  1.23 us (2%)
    pallas_call x1, Pallas kernels, per_device(): pl.pallas_call(kernel, in_specs=[pl.BlockSpec(memory_space=pltpu.HBM)] *...  47 us
    unnamed x1, local copies, waits for them, and re-layouts  1.23 us

profile of v2, /device:TPU:0, one launch (start us, length us, event | category | flops | bytes accessed | tf_op | source)
XLA Modules:
  0.0 52.5 jit_solution(1990704743916736218)
XLA Ops:
  2.6 47.0 %shard_map.149 = (f32[3,1,64]{2,1,0:T(1,128)}, f32[1,1]{1,0:T(1,128)}) custom-call(bf16[32,512,2,128]{3,2,1,0:T(2,128)(2,1)} %bitcast.8, f32[1,32]{1,0:T(1,128)} %occ_hbm.1, f32[4,8,65536]{2,1,0:T(8,128)} %ff_hbm.1, f32[3,65536]{1,0:T(4,128)} %g_hbm.1, s32[64]{0:T(128)} %spec_hbm.1, s32[4]{0:T(128)} %count_hbm.1, f32[4,8]{1,0:T(4,128)} %coup_hbm.1, ...), custom_call_target="tpu_custom_call" | custom-call | tf_op jit(solution)/shard_map/pallas_call | solution.py:502
  49.5 1.2 %copy.21 = f32[1,3,64]{2,0,1:T(1,128)} copy(f32[1,3,64]{2,0,1:T(1,128)} %bitcast.12) | data formatting | bytes 1536

commit v3 on v2

--- a/solution.py
+++ b/solution.py
@@ -14,6 +14,7 @@
 LANE = 128
 WIDE = 256
 CHUNKS = 8
+PUSHES = 16
 MESH = pl.DeviceIdType.MESH
 F32 = jnp.float32
 BF16 = jnp.bfloat16
@@ -77,6 +78,8 @@
     half_len = ff.shape[2]
     n_wide = half_len // WIDE
     step_tiles = tiles // CHUNKS
+    push_tiles = tiles // PUSHES
+    split = PUSHES // CHUNKS
     n_own = z_send.shape[0]
     own_rows = z_send.shape[1]
     own_atoms = own_rows // slots
@@ -144,7 +147,7 @@
     occ_part[...] = jnp.broadcast_to(jnp.where(here, jnp.concatenate([occ[...]] * (LANE // bands), axis=1), 0.0), (8, LANE))
 
     def wave_push(c):
-        at = pl.ds(c * step_tiles, step_tiles)
+        at = pl.ds(c * push_tiles, push_tiles)
         return pltpu.make_async_remote_copy(
             src_ref=w_send.at[:, at], dst_ref=w_all.at[side, :, at],
             send_sem=w_send_sem.at[c], recv_sem=w_recv_sem.at[c],
@@ -152,7 +155,7 @@
         )
 
     def wave_arrival(c):
-        at = pl.ds(c * step_tiles, step_tiles)
+        at = pl.ds(c * push_tiles, push_tiles)
         return pltpu.make_async_remote_copy(
             src_ref=w_send.at[:, at], dst_ref=w_all.at[1 - side, :, at],
             send_sem=w_send_sem.at[c], recv_sem=w_recv_sem.at[c],
@@ -166,20 +169,21 @@
 
     def widen_other(c):
         def one(t, carry):
-            at = c * step_tiles + t
+            at = c * push_tiles + t
             for b in range(blocks):
                 w_send[b, at] = raw_other[b, at].astype(F32)
             return carry
 
-        lax.fori_loop(0, step_tiles, one, 0, unroll=8)
+        lax.fori_loop(0, push_tiles, one, 0, unroll=8)
 
     for c in range(CHUNKS):
         for copy in wave_copies(raw_other, 1 - side, c, step_tiles, other_sem.at[c]):
             copy.wait()
-        widen_other(c)
-        if c == 0:
-            pl.semaphore_wait(barrier, 3 * group - 1)
-        wave_push(c).start()
+        for p in range(c * split, (c + 1) * split):
+            widen_other(p)
+            if p == 0:
+                pl.semaphore_wait(barrier, 3 * group - 1)
+            wave_push(p).start()
     occ_push.start()
 
     for copy in own_copies:
@@ -273,7 +277,7 @@
             waves_of_atoms(1, trig_b, j)
         wave_arrival(0).wait_recv()
         stage(0)
-        per_chunk = n_wide // CHUNKS
+        per_chunk = n_wide // PUSHES
 
         def pair(i, carry):
             k = 2 * i
@@ -463,7 +467,7 @@
         force_out[c] = result[c : c + 1, :atoms]
     energy_out[...] = energy
 
-    for c in range(CHUNKS):
+    for c in range(PUSHES):
         wave_push(c).wait_send()
     for q in range(n_own):
         pair_push(q).wait_send()
@@ -542,8 +546,8 @@
             dma(()),
             dma(()),
             dma(()),
-            dma((CHUNKS,)),
-            dma((CHUNKS,)),
+            dma((PUSHES,)),
+            dma((PUSHES,)),
             dma((2,)),
             dma((2, n_own)),
             dma((2, n_ga)),

time: 52.7 us -> 52.9 us (level)
  no operation moved by 1% of the time
where the time goes in v3:
time: 52.9 us; the launch traced here: 52.7 us
  Pallas kernels  47.1 us (89%)
  between operations  4.34 us (8%)
  local copies, waits for them, and re-layouts  1.23 us (2%)
    pallas_call x1, Pallas kernels, per_device(): pl.pallas_call(kernel, in_specs=[pl.BlockSpec(memory_space=pltpu.HBM)] *...  47.1 us
    unnamed x1, local copies, waits for them, and re-layouts  1.23 us

profile of v3, /device:TPU:0, one launch (start us, length us, event | category | flops | bytes accessed | tf_op | source)
XLA Modules:
  0.0 52.7 jit_solution(2830593096806831305)
XLA Ops:
  2.6 47.1 %shard_map.149 = (f32[3,1,64]{2,1,0:T(1,128)}, f32[1,1]{1,0:T(1,128)}) custom-call(bf16[32,512,2,128]{3,2,1,0:T(2,128)(2,1)} %bitcast.8, f32[1,32]{1,0:T(1,128)} %occ_hbm.1, f32[4,8,65536]{2,1,0:T(8,128)} %ff_hbm.1, f32[3,65536]{1,0:T(4,128)} %g_hbm.1, s32[64]{0:T(128)} %spec_hbm.1, s32[4]{0:T(128)} %count_hbm.1, f32[4,8]{1,0:T(4,128)} %coup_hbm.1, ...), custom_call_target="tpu_custom_call" | custom-call | tf_op jit(solution)/shard_map/pallas_call | solution.py:506
  49.7 1.2 %copy.21 = f32[1,3,64]{2,0,1:T(1,128)} copy(f32[1,3,64]{2,0,1:T(1,128)} %bitcast.12) | data formatting | bytes 1536
